TPU v7x, 256 devices: a whole 4x4x8 slice. The times are simulated.
256 devices in a mesh: wide: 64 (over y, z_lo, x), layer: 4 (over z_hi, core).
Axes of the slice: x: 4, y: 4, z: 8 (z_hi: 2, z_lo: 4; z = z_hi * 4 + z_lo), core: 2. Of those that a mesh axis runs over, the one named last changes fastest.
Arguments:
- factor: float32 [32768, 8192], P('layer', 'wide'), parts along dimension 0, may hold values from -1 to 21, as said below
Outputs:
- rotated: float32 [32768, 8192], P('layer', 'wide'), parts along dimension 0
- eigen_basis: float32 [32768, 8192], P('layer', 'wide'), parts along dimension 0
There are 4 independent parts, one for each index of `layer`. A program takes and returns all parts, laid end to end along the dimension named above; each array names one. Nothing has to cross between parts.
Inputs may be any that keep to these rules, and one draw needn't show every extreme that they name: `factor`: symmetric.
All inputs are finite; a program needn't handle non-finite values.
Results may differ from a plain program's by a relative error of at most 0.00095.
Values sent between devices are 32-bit elements; how exact they have to be, the bound alone decides.
A program may use at most 128 MiB of HBM per device.

v0:
```python
import jax
import jax.numpy as jnp
from jax import lax
from jax.sharding import Mesh
from jax.sharding import PartitionSpec as P

SWEEPS = 3
WIDE = ("wide_0", "wide_1", "wide_2")


floor_term = 0.01


def laid_out(parts, dim):
    dims = list(parts.shape[1:])
    dims[dim] *= parts.shape[0]
    return jnp.moveaxis(parts, 0, dim).reshape(dims)


def gather_in_order(shard, axes, order):
    parts = shard[None]
    for k in order:
        parts = lax.all_gather(parts, axes[k], axis=0, tiled=True)
    held = [lax.axis_size(axes[k]) for k in reversed(order)]
    parts = parts.reshape(*held, *shard.shape)
    turned = sorted(range(len(order)), key=lambda place: order[len(order) - 1 - place])
    return parts.transpose(*turned, *range(len(order), parts.ndim)).reshape(-1, *shard.shape)


def whole_of(shard, axes, order, dim):
    return laid_out(gather_in_order(shard, axes, order), dim)


def from_partner(shard, axis, bit):
    return lax.ppermute(shard, axis, [(i, i ^ 1 << bit) for i in range(lax.axis_size(axis))])


def cayley_sweeps(pair_block):
    order_size = pair_block.shape[0]
    identity_mat = jnp.eye(order_size, dtype=pair_block.dtype)
    rotation = identity_mat
    for repeat in range(SWEEPS):
        diagonal = jnp.diagonal(pair_block)
        spread = diagonal[None, :] - diagonal[:, None]
        ratios = (
            pair_block * spread / (spread * spread + 2.0 * pair_block * pair_block + floor_term)
        )
        skewed = 0.5 * (ratios - ratios.T) * (1.0 - identity_mat)
        half_turn = identity_mat + 0.5 * skewed
        system = identity_mat - 0.25 * jnp.dot(skewed, skewed, precision=lax.Precision.HIGHEST)
        lower_part = jnp.linalg.cholesky(system)
        square_turn = jnp.dot(half_turn, half_turn, precision=lax.Precision.HIGHEST)
        rotate_now = jax.scipy.linalg.cho_solve((lower_part, True), square_turn)
        pair_block = jnp.dot(
            rotate_now.T,
            jnp.dot(pair_block, rotate_now, precision=lax.Precision.HIGHEST),
            precision=lax.Precision.HIGHEST,
        )
        rotation = jnp.dot(rotation, rotate_now, precision=lax.Precision.HIGHEST)
    return rotation


def trade_rows(current, wide_count, width_half):
    order_size, pair_span = current.shape
    split_view = current.reshape(2, wide_count // 2, 2, width_half, pair_span)
    joined = jnp.concatenate([split_view[:, :, :1], split_view[::-1, :, 1:]], axis=2)
    return joined.reshape(order_size, pair_span)


def one_round(current, basis, my_pair):
    order_size, pair_span = current.shape
    pair_block = lax.dynamic_slice_in_dim(current, my_pair * pair_span, pair_span, 0)
    rotate = cayley_sweeps(pair_block)
    columns = jnp.dot(current, rotate, precision=lax.Precision.HIGHEST)
    pieces = whole_of(rotate[None], WIDE, (1, 0, 2), 0)
    how_many = pieces.shape[0]
    row_slab = columns
    row_slab = row_slab.reshape(how_many, pair_span, pair_span)
    updated = jnp.einsum("nba,nbc->nac", pieces, row_slab, precision=lax.Precision.HIGHEST)
    current = lax.dynamic_update_slice_in_dim(
        columns, updated.reshape(how_many * pair_span, pair_span), jnp.int32(0) * pair_span, 0
    )
    basis = jnp.dot(basis, rotate, precision=lax.Precision.HIGHEST)
    return (current, basis)


def body(factor):
    wide_count = lax.axis_size(WIDE)
    my_pair = lax.axis_index(WIDE)
    order_size, pair_span = factor.shape
    width_half = pair_span // 2
    row_index = lax.broadcasted_iota(jnp.int32, (order_size, pair_span), 0)
    col_index = lax.broadcasted_iota(jnp.int32, (order_size, pair_span), 1) + my_pair * pair_span
    basis = (row_index == col_index).astype(jnp.float32)
    current = factor
    for repeat in range(2):
        if repeat == 1:
            moved_factor, moved_basis = from_partner(
                (current[:, width_half:], basis[:, width_half:]), WIDE, wide_count.bit_length() - 2
            )
            current = jnp.concatenate([current[:, :width_half], moved_factor], axis=1)
            basis = jnp.concatenate([basis[:, :width_half], moved_basis], axis=1)
            current = trade_rows(current, wide_count, width_half)
        current, basis = one_round(current, basis, my_pair)
    return (current, basis)


def solution(mesh):
    finer = Mesh(
        mesh.devices.reshape(4, 4, 4, mesh.shape["layer"]), ("wide_0", "wide_1", "wide_2", "layer")
    )
    in_specs = (P("layer", WIDE),)
    out_specs = (P("layer", WIDE), P("layer", WIDE))
    return jax.shard_map(body, mesh=finer, in_specs=in_specs, out_specs=out_specs, check_vma=False)
```

profile of v0, /device:TPU:2, one launch (start us, length us, event | category | flops | bytes accessed | tf_op | source)
XLA Modules:
  0.0 474.4 jit_solution(8822284381728006457)
XLA Ops:
  10.3 11.7 %cholesky.104 = f32[128,128]{1,0:T(8,128)S(1)} custom-call(f32[128,128]{1,0:T(8,128)S(1)} %fusion.100), custom_call_target="Cholesky" | custom-call | tf_op jit(solution)/shard_map/jit(cholesky)/cholesky | solution.py:51
  23.4 9.8 %custom-call.24 = f32[1,128,128]{1,2,0:T(8,128)S(1)} custom-call(f32[1,128,128]{2,1,0:T(8,128)S(1)} %fusion.18), custom_call_target="InvertDiagBlocksLowerTriangular" | custom-call | tf_op jit(solution)/shard_map/jit(_cho_solve)/triangular_solve | solution.py:53
  36.7 11.7 %cholesky.115 = f32[128,128]{1,0:T(8,128)S(1)} custom-call(f32[128,128]{1,0:T(8,128)S(1)} %fusion.95), custom_call_target="Cholesky" | custom-call | tf_op jit(solution)/shard_map/jit(cholesky)/cholesky | solution.py:51
  49.8 9.8 %custom-call.25 = f32[1,128,128]{1,2,0:T(8,128)S(1)} custom-call(f32[1,128,128]{2,1,0:T(8,128)S(1)} %fusion.19), custom_call_target="InvertDiagBlocksLowerTriangular" | custom-call | tf_op jit(solution)/shard_map/jit(_cho_solve)/triangular_solve | solution.py:53
  63.1 11.7 %cholesky.126 = f32[128,128]{1,0:T(8,128)S(1)} custom-call(f32[128,128]{1,0:T(8,128)S(1)} %fusion.90), custom_call_target="Cholesky" | custom-call | tf_op jit(solution)/shard_map/jit(cholesky)/cholesky | solution.py:51
  76.2 9.8 %custom-call.26 = f32[1,128,128]{1,2,0:T(8,128)S(1)} custom-call(f32[1,128,128]{2,1,0:T(8,128)S(1)} %fusion.20), custom_call_target="InvertDiagBlocksLowerTriangular" | custom-call | tf_op jit(solution)/shard_map/jit(_cho_solve)/triangular_solve | solution.py:53
  86.7 15.6 %all-gather = f32[512,128]{1,0:T(8,128)} all-gather(f32[128,128]{1,0:T(8,128)S(1)} %fusion.147), channel_id=2, replica_groups=mesh['wide_0'=4,'wide_1'=4,'wide_2'=4,'layer'=4] {'wide_1'}, dimensions={0}, use_global_device_ids=true | all-gather | bytes 327680 | tf_op jit(solution)/shard_map/all_gather | solution.py:23
  102.3 28.8 %all-gather.7.cloned.1.call-done = f32[16,1,128,128]{3,2,1,0:T(8,128)} async-done(((f32[4,1,128,128]{3,2,1,0:T(8,128)}), f32[16,1,128,128]{3,2,1,0:T(8,128)}) %all-gather.7.cloned.1.call-update) | async-done | bytes 1048592 | tf_op jit(solution)/shard_map/all_gather | solution.py:23
  131.2 8.1 %convolution_bitcast_fusion = f32[8192,128]{0,1:T(8,128)} fusion(f32[128,128]{1,0:T(8,128)S(1)} %fusion.147, f32[8192,128]{1,0:T(8,128)} %param.4), kind=kOutput, calls=%fused_computation.6 | convolution fusion | flops 1610612736 | bytes 8454144 | tf_op jit(solution)/shard_map/dot_general | solution.py:74
  139.3 6.0 %copy.106 = f32[8192,128]{1,0:T(8,128)} copy(f32[8192,128]{0,1:T(8,128)} %convolution_bitcast_fusion) | data formatting | bytes 8388608 | tf_op jit(solution)/shard_map/reshape | solution.py:78
  145.2 38.2 %all-gather.9.cloned.1.call-done = f32[64,1,128,128]{3,2,1,0:T(8,128)} async-done(((f32[16,1,128,128]{3,2,1,0:T(8,128)}), f32[64,1,128,128]{3,2,1,0:T(8,128)}) %all-gather.9.cloned.1.call-update) | async-done | bytes 4194320 | tf_op jit(solution)/shard_map/all_gather | solution.py:23
  183.4 5.2 %copy.80 = f32[4,4,4,1,128,128]{4,5,0,2,1,3:T(8,128)} copy(f32[4,4,4,1,128,128]{5,4,2,1,0,3:T(8,128)} %bitcast.185) | data formatting | bytes 8388608 | tf_op jit(solution)/shard_map/reshape | solution.py:25
  188.6 6.6 %fusion.148 = f32[64,128,128]{2,1,0:T(8,128)S(1)} fusion(f32[64,128,128]{1,2,0:T(8,128)} %bitcast.181, f32[64,128,128]{2,1,0:T(8,128)} %bitcast.179), kind=kOutput, calls=%fused_computation.227 | convolution fusion | flops 1610612736 | bytes 12582912 | tf_op jit(solution)/shard_map/nba,nbc->nac/dot_general | solution.py:79
  195.3 4.7 fusion.141
  200.0 2.8 copy.82
  202.8 3.1 collective-permute-start
  205.9 45.8 %collective-permute-done = f32[8192,64]{0,1:T(8,128)} collective-permute-done((f32[8192,64]{0,1:T(8,128)S(1)}, f32[8192,64]{0,1:T(8,128)}, u32[]{:S(2)}, u32[]{:S(2)}) %collective-permute-start) | collective-permute-done | bytes 2097184 | tf_op jit(solution)/shard_map/ppermute | solution.py:35
  251.7 3.8 copy.83
  255.6 4.6 pad_maximum_fusion
  270.1 11.7 %cholesky.137 = f32[128,128]{1,0:T(8,128)S(1)} custom-call(f32[128,128]{1,0:T(8,128)S(1)} %fusion.84), custom_call_target="Cholesky" | custom-call | tf_op jit(solution)/shard_map/jit(cholesky)/cholesky | solution.py:51
  283.2 9.8 %custom-call.27 = f32[1,128,128]{1,2,0:T(8,128)S(1)} custom-call(f32[1,128,128]{2,1,0:T(8,128)S(1)} %fusion.21), custom_call_target="InvertDiagBlocksLowerTriangular" | custom-call | tf_op jit(solution)/shard_map/jit(_cho_solve)/triangular_solve | solution.py:53
  296.5 11.7 %cholesky.148 = f32[128,128]{1,0:T(8,128)S(1)} custom-call(f32[128,128]{1,0:T(8,128)S(1)} %fusion.79), custom_call_target="Cholesky" | custom-call | tf_op jit(solution)/shard_map/jit(cholesky)/cholesky | solution.py:51
  309.6 9.8 %custom-call.28 = f32[1,128,128]{1,2,0:T(8,128)S(1)} custom-call(f32[1,128,128]{2,1,0:T(8,128)S(1)} %fusion.22), custom_call_target="InvertDiagBlocksLowerTriangular" | custom-call | tf_op jit(solution)/shard_map/jit(_cho_solve)/triangular_solve | solution.py:53
  322.9 11.7 %cholesky.159 = f32[128,128]{1,0:T(8,128)S(1)} custom-call(f32[128,128]{1,0:T(8,128)S(1)} %fusion.74), custom_call_target="Cholesky" | custom-call | tf_op jit(solution)/shard_map/jit(cholesky)/cholesky | solution.py:51
  336.0 9.8 %custom-call.29 = f32[1,128,128]{1,2,0:T(8,128)S(1)} custom-call(f32[1,128,128]{2,1,0:T(8,128)S(1)} %fusion.23), custom_call_target="InvertDiagBlocksLowerTriangular" | custom-call | tf_op jit(solution)/shard_map/jit(_cho_solve)/triangular_solve | solution.py:53
  346.5 14.8 %all-gather.1 = f32[512,128]{1,0:T(8,128)} all-gather(f32[128,128]{1,0:T(8,128)S(1)} %fusion.154), channel_id=3, replica_groups=mesh['wide_0'=4,'wide_1'=4,'wide_2'=4,'layer'=4] {'wide_1'}, dimensions={0}, use_global_device_ids=true | all-gather | bytes 327680 | tf_op jit(solution)/shard_map/all_gather | solution.py:23
  361.3 28.1 %all-gather.11.cloned.1.call-done = f32[16,1,128,128]{3,2,1,0:T(8,128)} async-done(((f32[4,1,128,128]{3,2,1,0:T(8,128)}), f32[16,1,128,128]{3,2,1,0:T(8,128)}) %all-gather.11.cloned.1.call-update) | async-done | bytes 1048592 | tf_op jit(solution)/shard_map/all_gather | solution.py:23
  394.2 44.7 %collective-permute-done.1 = f32[8192,64]{0,1:T(8,128)S(1)} collective-permute-done((f32[8192,64]{0,1:T(8,128)S(1)}, f32[8192,64]{0,1:T(8,128)S(1)}, u32[]{:S(2)}, u32[]{:S(2)}) %collective-permute-start.1) | collective-permute-done | bytes 2097184 | tf_op jit(solution)/shard_map/ppermute | solution.py:35
  438.9 8.5 %fusion = f32[8192,128]{1,0:T(8,128)} fusion(f32[128,128]{1,0:T(8,128)S(1)} %fusion.154, f32[8192,64]{0,1:T(8,128)S(1)} %collective-permute-done.1, f32[8192,64]{0,1:T(8,128)S(1)} %get-tuple-element.4), kind=kOutput, calls=%fused_computation.9 | convolution fusion | flops 1611661312 | bytes 8454144 | tf_op jit(solution)/shard_map/dot_general | solution.py:83
  447.4 4.9 %fusion.68 = f32[64,128,128]{2,1,0:T(8,128)} fusion(f32[64,128,128]{2,1,0:T(8,128)S(1)} %bitcast.178, f32[128,128]{1,0:T(8,128)S(1)} %fusion.154), kind=kOutput, calls=%fused_computation.127 | convolution fusion | flops 1610612736 | bytes 8454144 | tf_op jit(solution)/shard_map/dot_general | solution.py:74
  452.3 5.2 %copy.99 = f32[4,4,4,1,128,128]{4,5,0,2,1,3:T(8,128)} copy(f32[4,4,4,1,128,128]{5,4,2,1,0,3:T(8,128)} %bitcast.184) | data formatting | bytes 8388608 | tf_op jit(solution)/shard_map/reshape | solution.py:25
  457.6 9.9 %fusion.155 = f32[64,128,128]{2,1,0:T(8,128)} fusion(f32[64,128,128]{1,2,0:T(8,128)} %bitcast.182, f32[64,128,128]{2,1,0:T(8,128)} %fusion.68), kind=kOutput, calls=%fused_computation.234 | convolution fusion | flops 1610612736 | bytes 12582912 | tf_op jit(solution)/shard_map/nba,nbc->nac/dot_general | solution.py:79
  (111 shorter events, 41.0 us)
Async XLA Ops:
  7.2 123.9 %all-gather.7.cloned.1.call-start = ((), (), s32[]{:S(2)}) async-start(), calls=%async_computation | async-start | bytes 1310720 | tf_op jit(solution)/shard_map/all_gather | solution.py:23
  102.3 81.1 %all-gather.9.cloned.1.call-start = ((), (), s32[]{:S(2)}) async-start(), calls=%async_computation.1 | async-start | bytes 5242880 | tf_op jit(solution)/shard_map/all_gather | solution.py:23
  131.1 258.3 %all-gather.11.cloned.1.call-start = ((), (), s32[]{:S(2)}) async-start(), calls=%async_computation.2 | async-start | bytes 1310720 | tf_op jit(solution)/shard_map/all_gather | solution.py:23
  202.8 48.9 %collective-permute-start = (f32[8192,64]{0,1:T(8,128)S(1)}, f32[8192,64]{0,1:T(8,128)}, u32[]{:S(2)}, u32[]{:S(2)}) collective-permute-start(f32[8192,64]{0,1:T(8,128)S(1)} %copy.82), channel_id=1, source_target_pairs={{0,128},{4,132},{8,136},{12,140},{16,144},{20,148},{24,152},{28,15... | collective-permute-start | bytes 6291464 | tf_op jit(solution)/shard_map/ppermute | solution.py:35
  265.9 2.0 copy-start
  361.3 91.0 %all-gather.13.cloned.1.call-start = ((), (), s32[]{:S(2)}) async-start(), calls=%async_computation.3 | async-start | bytes 5242880 | tf_op jit(solution)/shard_map/all_gather | solution.py:23
  392.0 46.9 %collective-permute-start.1 = (f32[8192,64]{0,1:T(8,128)S(1)}, f32[8192,64]{0,1:T(8,128)S(1)}, u32[]{:S(2)}, u32[]{:S(2)}) collective-permute-start(f32[8192,64]{0,1:T(8,128)S(1)} %get-tuple-element.5), channel_id=1, source_target_pairs={{0,128},{4,132},{8,136},{12,140},{16,144},{20,148},{24,152},{28,15... | collective-permute-start | bytes 6291464 | tf_op jit(solution)/shard_map/ppermute | solution.py:35
  438.9 8.5 %copy-start.1 = (f32[2,32,2,64,128]{4,3,2,1,0:T(8,128)S(1)}, f32[2,32,2,64,128]{4,3,2,1,0:T(8,128)}, u32[]{:S(2)}) copy-start(f32[2,32,2,64,128]{4,3,2,1,0:T(8,128)} %copy-done) | copy-start | bytes 12582916
Sparse Core Ops, SparseCore 0:
  102.4 28.6 all-gather.6
  132.9 50.4 all-gather.8
  361.4 27.9 all-gather.10
  391.1 50.4 all-gather.12
where the time goes:
time: 481 us; the launch traced here: 474 us
  waiting for transfers between devices  186 us (39%)
  other arithmetic  145 us (30%)
  matrix products  49.3 us (10%)
  local copies, waits for them, and re-layouts  43.8 us (9%)
  blocking collectives  30.3 us (6%)
  between operations  14.9 us (3%)
  starting transfers between devices  5.42 us (1%)
    all_gather x4, waiting for transfers between devices, gather_in_order(): parts = lax.all_gather(parts, axes[k], axis=0, tiled=True)  95.1 us
    ppermute x2, waiting for transfers between devices, from_partner(): lax.ppermute(shard, axis, [(i, i ^ 1 << bit) for i in range(lax.axis_size...  90.5 us
    another operation x18, other arithmetic, cayley_sweeps(): lower_part = jnp.linalg.cholesky(system)  74.3 us
    another operation x12, other arithmetic, cayley_sweeps(): rotate_now = jax.scipy.linalg.cho_solve((lower_part, True), square_turn)  62.8 us
    all_gather x2, blocking collectives, gather_in_order(): parts = lax.all_gather(parts, axes[k], axis=0, tiled=True)  30.3 us
    dot_general x2, matrix products, one_round(): jnp.einsum('nba,nbc->nac', pieces, row_slab, precision=lax.Precision.HIGH...  16.5 us
    dot_general x2, matrix products, one_round(): columns = jnp.dot(current, rotate, precision=lax.Precision.HIGHEST)  13 us
    dot_general x2, matrix products, one_round(): basis = jnp.dot(basis, rotate, precision=lax.Precision.HIGHEST)  10.7 us
  transfers between devices with their start and end apart: 6, of which 5 were waited for; matrix products, arithmetic and copies ran while one was open for 6% of the time, Pallas kernels for 0%

commit v1 on v0

v1 whole, which is shorter than its diff:
```python
import functools

import jax
import jax.numpy as jnp
from jax import lax
from jax.experimental import pallas as pl
from jax.experimental.pallas import tpu as pltpu
from jax.sharding import PartitionSpec as P

SWEEPS = 3
f32, bf16 = jnp.float32, jnp.bfloat16
floor_term = 0.01
HBM = pl.BlockSpec(memory_space=pl.ANY)
VMEM = pl.BlockSpec(memory_space=pltpu.VMEM)


def dot(a, b):
    return jnp.dot(a, b, precision=lax.Precision.HIGHEST, preferred_element_type=f32)


def split(a):
    high = a.astype(bf16)
    return high, (a - high.astype(f32)).astype(bf16)


def paired(b):
    high, low = split(b)
    return jnp.concatenate(
        [
            jnp.concatenate([high, low], axis=1),
            jnp.concatenate([high, jnp.zeros_like(low)], axis=1),
        ],
        axis=0,
    )


def dot_paired(a, b_paired):
    both = jnp.dot(jnp.concatenate(split(a), axis=1), b_paired, preferred_element_type=f32)
    half = both.shape[1] // 2
    return both[:, :half] + both[:, half:]


def dot_three(a, b):
    return dot_paired(a, paired(b))


def rotation(block):
    size = block.shape[0]
    row = lax.broadcasted_iota(jnp.int32, (size, size), 0)
    eye = (row == lax.broadcasted_iota(jnp.int32, (size, size), 1)).astype(f32)

    def sweep(_, carry):
        m, q = carry
        on = m * eye
        spread = jnp.sum(on, axis=0, keepdims=True) - jnp.sum(on, axis=1, keepdims=True)
        ratio = m * spread / (spread * spread + 2.0 * m * m + floor_term)
        k = 0.5 * (ratio - ratio.T)
        square = dot(k, k)
        bound = jnp.sum(jnp.abs(square), axis=0, keepdims=True)
        bound = 0.25 * 1.001 * jnp.max(bound, axis=1, keepdims=True)
        scale = 2.0 / (2.0 + bound)
        reach = bound / (2.0 + bound)
        e = eye * (1.0 - scale) + (0.25 * scale) * square
        p = 2.0 * scale * eye + scale * k

        def step(c):
            p, e, reach, _ = c
            w = 2.0 / (2.0 - reach * reach)
            both = dot_three(jnp.concatenate([p, e], axis=0), e)
            reach = reach * reach / (2.0 - reach * reach)
            return w * (p + both[:size]), eye * (1.0 - w) + w * both[size:], reach, jnp.max(reach)

        p, *_ = lax.while_loop(lambda c: c[3] > 1e-7, step, (p, e, reach, jnp.max(reach)))
        rest = 2.0 * eye - p + 0.5 * dot(k, p)
        g = p + 0.5 * dot_three(p, rest) - eye
        both = dot(jnp.concatenate([m, q], axis=0), g)
        return dot(g.T, both[:size]), both[size:]

    return lax.fori_loop(0, SWEEPS, sweep, (block, eye))


def my_rows(span):
    return pl.ds(pl.multiple_of(lax.axis_index("wide") * span, span), span)


def first_kernel(whole_ref, block_ref, q_ref, note_ref, send_ref, keep_ref, m_ref, w_ref, sem):
    span = q_ref.shape[0]
    half = span // 2

    @pl.when(pl.program_id(0) == 0)
    def _():
        copy = pltpu.make_async_copy(whole_ref.at[my_rows(span)], m_ref, sem)
        copy.start()
        copy.wait()
        m, q = rotation(m_ref[...])
        q_ref[...] = q
        note_ref[:half] = q.T[half:]
        note_ref[half:] = m[half:]
        m_ref[...] = m
        w_ref[0] = paired(jnp.concatenate([q[:, half:], q[:, :half]], axis=1))
        w_ref[1] = paired(q)

    top = dot_paired(block_ref[0], w_ref[0])
    bottom = dot_paired(block_ref[1], w_ref[1])
    low = lax.broadcasted_iota(jnp.int32, top.shape, 1) < half
    send_ref[...] = jnp.where(low, top, bottom)
    keep_ref[...] = jnp.where(low, bottom, top)


def first_round(factor, rows):
    order, span = factor.shape
    square = jax.ShapeDtypeStruct((span, span), f32)
    packed = jax.ShapeDtypeStruct((order // 2, span), f32)
    fixed = pl.BlockSpec((span, span), lambda i: (0, 0))
    moving = pl.BlockSpec((rows, span), lambda i: (i, 0))
    return pl.pallas_call(
        first_kernel,
        grid=(order // 2 // rows,),
        out_shape=(square, square, packed, packed, square),
        in_specs=[HBM, pl.BlockSpec((2, rows, span), lambda i: (0, i, 0))],
        out_specs=[fixed, fixed, moving, moving, fixed],
        scratch_shapes=[
            pltpu.VMEM((2, 2 * span, 2 * span), bf16),
            pltpu.SemaphoreType.DMA,
        ],
        cost_estimate=pl.CostEstimate(flops=3 * 10**9, bytes_accessed=10**7, transcendentals=0),
        name="first_round",
    )(factor, factor.reshape(2, order // 2, span))


def second_kernel(pairs, whole_ref, q_ref, m_ref, note_ref, turn_ref, wt_ref, w_ref, cross_ref, sem):
    span = q_ref.shape[0]
    half = span // 2
    mine = lax.axis_index("wide")
    other = lax.rem(mine + pairs // 2, pairs)
    copy = pltpu.make_async_copy(
        whole_ref.at[pl.ds(pl.multiple_of(other * span, span), span)], cross_ref, sem
    )
    copy.start()
    copy.wait()
    q = q_ref[...]
    qt = q.T
    note = note_ref[...]
    across = dot(note[:half], dot(cross_ref[...], q))[:, :half]
    m = m_ref[...]
    block = jnp.concatenate(
        [
            jnp.concatenate([m[:half, :half], across.T], axis=1),
            jnp.concatenate([across, note[half:, half:]], axis=1),
        ],
        axis=0,
    )
    _, turn = rotation(block)
    turn_ref[...] = turn
    turned = turn.T
    here = dot(turned[:, :half], qt[:half])
    there = dot(turned[:, half:], note[:half])
    low = mine < pairs // 2
    wt_ref[:, :span] = jnp.where(low, here, there)
    wt_ref[:, span:] = jnp.where(low, there, here)
    w_ref[0] = here.T
    w_ref[1] = there.T


def second_round(factor, q, m, note):
    order, span = factor.shape
    return pl.pallas_call(
        functools.partial(second_kernel, order // span),
        out_shape=(
            jax.ShapeDtypeStruct((span, span), f32),
            jax.ShapeDtypeStruct((span, 2 * span), f32),
            jax.ShapeDtypeStruct((2, span, span), f32),
        ),
        in_specs=[HBM, VMEM, VMEM, VMEM],
        out_specs=[VMEM, VMEM, VMEM],
        scratch_shapes=[pltpu.VMEM((span, span), f32), pltpu.SemaphoreType.DMA],
        cost_estimate=pl.CostEstimate(flops=2 * 10**9, bytes_accessed=10**6, transcendentals=0),
        name="second_round",
    )(factor, q, m, note)


def last_kernel(recv_ref, keep_ref, turn_ref, wt_ref, out_ref, turn_pair):
    span = turn_ref.shape[0]
    half = span // 2

    @pl.when(pl.program_id(0) == 0)
    def _():
        turn = turn_ref[...]
        turn_pair[0] = paired(jnp.concatenate([turn[half:], turn[:half]], axis=0))
        turn_pair[1] = paired(turn)

    recv, keep = recv_ref[...], keep_ref[...]
    low = lax.broadcasted_iota(jnp.int32, recv.shape, 1) < half
    top = dot_paired(jnp.where(low, recv, keep), turn_pair[0])
    bottom = dot_paired(jnp.where(low, keep, recv), turn_pair[1])
    for b in range(wt_ref.shape[1]):
        rows = slice(b * span, (b + 1) * span)
        z_high, z_low = split(jnp.concatenate([top[rows], bottom[rows]], axis=0))
        w_high, w_low = split(jnp.concatenate([wt_ref[0, b], wt_ref[1, b]], axis=0))
        both = jnp.dot(
            w_high, jnp.concatenate([z_high, z_low], axis=1), preferred_element_type=f32
        )
        out = both[:, :span] + both[:, span:] + jnp.dot(w_low, z_high, preferred_element_type=f32)
        out_ref[0, rows] = out[:span]
        out_ref[1, rows] = out[span:]


def last_step(recv, keep, turn, wt, at_once):
    rows, span = recv.shape
    rows_now = at_once * span
    moving = pl.BlockSpec((rows_now, span), lambda i: (i, 0))
    out = pl.pallas_call(
        last_kernel,
        grid=(rows // rows_now,),
        out_shape=jax.ShapeDtypeStruct((2, rows, span), f32),
        in_specs=[
            moving,
            moving,
            pl.BlockSpec((span, span), lambda i: (0, 0)),
            pl.BlockSpec((2, at_once, span, 2 * span), lambda i: (0, i, 0, 0)),
        ],
        out_specs=pl.BlockSpec((2, rows_now, span), lambda i: (0, i, 0)),
        scratch_shapes=[pltpu.VMEM((2, 2 * span, 2 * span), bf16)],
        cost_estimate=pl.CostEstimate(flops=3 * 10**9, bytes_accessed=10**7, transcendentals=0),
        name="last_step",
    )(recv, keep, turn, wt.reshape(2, -1, span, 2 * span))
    return out.reshape(2 * rows, span)


def body(pairs, factor):
    order, span = factor.shape
    mine = lax.axis_index("wide")
    other = lax.rem(mine + pairs // 2, pairs)
    partners = [(i, (i + pairs // 2) % pairs) for i in range(pairs)]
    q, note, send, keep, m = first_round(factor, 512)
    note = lax.ppermute(note, "wide", partners)
    recv = lax.ppermute(send, "wide", partners)
    turn, wt, w = second_round(factor, q, m, note)
    basis = jnp.zeros((order, span), f32)
    basis = lax.dynamic_update_slice_in_dim(basis, w[0], mine * span, 0)
    basis = lax.dynamic_update_slice_in_dim(basis, w[1], other * span, 0)
    rotated = last_step(recv, keep, turn, lax.all_gather(wt, "wide"), 2)
    return rotated, basis


def solution(mesh):
    spec = P("layer", "wide")
    return jax.shard_map(
        functools.partial(body, mesh.shape["wide"]),
        mesh=mesh,
        in_specs=(spec,),
        out_specs=(spec, spec),
        check_vma=False,
    )
```

time: 481 us -> 427 us (0.89); the launches traced: 474 us -> 426 us
  waiting for transfers between devices: 186 us -> 360 us
  other arithmetic: 145 us -> 0 us
  matrix products: 49.3 us -> 0 us
  Pallas kernels: 0 us -> 40.6 us
  local copies, waits for them, and re-layouts: 43.8 us -> 4.18 us
  blocking collectives: 30.3 us -> 0 us
    all_gather x4 -> x1, waiting for transfers between devices: 95.1 us -> 316 us  [body(): rotated = last_step(recv, keep, turn, lax.all_gather(wt, 'wide'), 2)]
    another operation x30 -> x0, other arithmetic: 137 us -> none  [the longest x18 74.3 us: cayley_sweeps(): lower_part = jnp.linalg.cholesky(system)]
    ppermute x2, waiting for transfers between devices: 90.5 us -> 44 us  [the longest x1 41.2 us: body(): recv = lax.ppermute(send, 'wide', partners)]
    dot_general x32 -> x0, matrix products: 46.4 us -> none  [the longest x2 16.5 us: one_round(): jnp.einsum('nba,nbc->nac', pieces, row_slab, precision=lax.Precision.HIGH...]
    pallas_call x0 -> x3, Pallas kernels: none -> 40.6 us  [the longest x1 15.5 us: first_round(): pl.pallas_call(first_kernel, grid=(order // 2 // rows,), out_shape=(squar...]
    all_gather x2 -> x0, blocking collectives: 30.3 us -> none  [gather_in_order(): parts = lax.all_gather(parts, axes[k], axis=0, tiled=True)]
    reshape x3 -> x0, local copies, waits for them, and re-layouts: 16.4 us -> none  [the longest x2 10.5 us: gather_in_order(): parts = parts.reshape(*held, *shard.shape)]
    slice x4 -> x0, local copies, waits for them, and re-layouts: 9.62 us -> none  [the longest x1 4.71 us: body(): current = jnp.concatenate([current[:, :width_half], moved_factor], axis=1)]
  transfers between devices with their start and end apart: 6 -> 3, of which waited for: 5 -> 3; matrix products, arithmetic and copies ran while one was open for 6% -> 1% of each run, Pallas kernels for 0% -> 0%
where the time goes in v1:
time: 427 us; the launch traced here: 426 us
  waiting for transfers between devices  360 us (84%)
  Pallas kernels  40.6 us (10%)
  between operations  14.1 us (3%)
  starting transfers between devices  6.59 us (2%)
    all_gather x1, waiting for transfers between devices, body(): rotated = last_step(recv, keep, turn, lax.all_gather(wt, 'wide'), 2)  316 us
    ppermute x1, waiting for transfers between devices, body(): recv = lax.ppermute(send, 'wide', partners)  41.2 us
    pallas_call x1, Pallas kernels, first_round(): pl.pallas_call(first_kernel, grid=(order // 2 // rows,), out_shape=(squar...  15.5 us
    pallas_call x1, Pallas kernels, last_step(): pl.pallas_call(last_kernel, grid=(rows // rows_now,), out_shape=jax.Shape...  15.4 us
    pallas_call x1, Pallas kernels, second_round(): pl.pallas_call(functools.partial(second_kernel, order // span), out_shape...  9.65 us
  transfers between devices with their start and end apart: 3, of which 3 were waited for; matrix products, arithmetic and copies ran while one was open for 1% of the time, Pallas kernels for 0%

profile of v1, /device:TPU:2, one launch (start us, length us, event | category | flops | bytes accessed | tf_op | source)
XLA Modules:
  0.0 425.6 jit_solution(9627568321512811180)
XLA Ops:
  7.2 0.0 all-gather.3.cloned.1.call-start
  7.2 15.5 %first_round.1 = (f32[128,128]{1,0:T(8,128)}, f32[128,128]{1,0:T(8,128)}, f32[4096,128]{1,0:T(8,128)}, f32[4096,128]{1,0:T(8,128)}, f32[128,128]{1,0:T(8,128)}) custom-call(f32[8192,128]{1,0:T(8,128)} %whole_ref.3, f32[2,4096,128]{2,1,0:T(8,128)} %bitcast.9), custom_call_target="tpu_custom_call" | custom-call | flops 3000000000 | bytes 10000000 | tf_op jit(solution)/shard_map/first_round/pallas_call | solution.py:116
  22.7 3.3 collective-permute-start.1
  26.0 2.8 collective-permute-done.1.note_ref
  28.8 0.0 copy-start.2
  28.8 0.6 copy-done.2
  29.4 9.6 %second_round.1 = (f32[128,128]{1,0:T(8,128)}, f32[128,256]{1,0:T(8,128)}, f32[2,128,128]{2,1,0:T(8,128)}) custom-call(f32[8192,128]{1,0:T(8,128)} %whole_ref.3, f32[128,128]{1,0:T(8,128)} %get-tuple-element.12.q_ref, f32[128,128]{1,0:T(8,128)} %get-tuple-element.13.m_ref, f32[128,128]{1,0:T(8,128)} %copy-done.2), custom_call_target="tpu_custom_call" | custom-call | flops 2000000000 | bytes 1000000 | tf_op jit(solution)/shard_map/second_round/pallas_call | solution.py:167
  39.1 0.0 copy-start.1
  39.1 0.0 all-gather.3.cloned.1.call-update
  39.1 3.3 collective-permute-start
  42.4 2.3 broadcast_in_dim.3
  44.7 0.0 copy-done.1
  44.7 0.6 bitcast_dynamic-update-slice_fusion.1
  45.3 0.6 bitcast_dynamic-update-slice_fusion
  46.0 41.2 %collective-permute-done.recv_ref = f32[4096,128]{1,0:T(8,128)S(1)} collective-permute-done((f32[4096,128]{1,0:T(8,128)}, f32[4096,128]{1,0:T(8,128)S(1)}, u32[]{:S(2)}, u32[]{:S(2)}) %collective-permute-start) | collective-permute-done | bytes 2097184 | tf_op jit(solution)/shard_map/ppermute | solution.py:237
  87.1 0.0 copy-start
  87.1 316.3 %all-gather.3.cloned.1.call-done = f32[8192,256]{1,0:T(8,128)} async-done(((f32[128,256]{1,0:T(8,128)}), f32[8192,256]{1,0:T(8,128)}) %all-gather.3.cloned.1.call-update) | async-done | bytes 8388624 | tf_op jit(solution)/shard_map/all_gather | solution.py:242
  403.4 0.0 copy-done
  403.4 15.4 %last_step.1 = f32[2,4096,128]{2,1,0:T(8,128)} custom-call(f32[4096,128]{1,0:T(8,128)} %copy-done, f32[4096,128]{1,0:T(8,128)} %get-tuple-element.11.keep_ref, f32[128,128]{1,0:T(8,128)} %get-tuple-element.15.turn_ref, f32[2,32,128,256]{3,2,1,0:T(8,128)} %bitcast.7), custom_call_target="tpu_custom_call" | custom-call | flops 3000000000 | bytes 10000000 | tf_op jit(solution)/shard_map/last_step/pallas_call | solution.py:212
Async XLA Ops:
  7.2 396.2 %all-gather.3.cloned.1.call-start = ((), (), s32[]{:S(2)}) async-start(), calls=%async_computation | async-start | bytes 8519680 | tf_op jit(solution)/shard_map/all_gather | solution.py:242
  22.7 6.1 %collective-permute-start.1 = (f32[128,128]{1,0:T(8,128)}, f32[128,128]{1,0:T(8,128)S(1)}, u32[]{:S(2)}, u32[]{:S(2)}) collective-permute-start(f32[128,128]{1,0:T(8,128)} %get-tuple-element.14), channel_id=1, source_target_pairs={{0,128},{4,132},{8,136},{12,140},{16,144},{20,148},{24,152},{28,15... | collective-permute-start | bytes 196616 | tf_op jit(solution)/shard_map/ppermute | solution.py:236
  28.8 0.6 copy-start.2
  39.1 5.6 %copy-start.1 = (f32[2,128,128]{2,1,0:T(8,128)S(1)}, f32[2,128,128]{2,1,0:T(8,128)}, u32[]{:S(2)}) copy-start(f32[2,128,128]{2,1,0:T(8,128)} %get-tuple-element.17) | copy-start | bytes 393220
  39.1 48.0 %collective-permute-start = (f32[4096,128]{1,0:T(8,128)}, f32[4096,128]{1,0:T(8,128)S(1)}, u32[]{:S(2)}, u32[]{:S(2)}) collective-permute-start(f32[4096,128]{1,0:T(8,128)} %get-tuple-element.10), channel_id=1, source_target_pairs={{0,128},{4,132},{8,136},{12,140},{16,144},{20,148},{24,152},{28,15... | collective-permute-start | bytes 6291464 | tf_op jit(solution)/shard_map/ppermute | solution.py:237
  87.1 316.3 %copy-start = (f32[4096,128]{1,0:T(8,128)}, f32[4096,128]{1,0:T(8,128)S(1)}, u32[]{:S(2)}) copy-start(f32[4096,128]{1,0:T(8,128)S(1)} %collective-permute-done.recv_ref) | copy-start | bytes 6291460
Sparse Core Ops, SparseCore 0:
  39.2 364.0 all-gather.2

commit v2 on v1

v2 whole, which is shorter than its diff:
```python
import functools

import jax
import jax.numpy as jnp
from jax import lax
from jax.experimental import pallas as pl
from jax.experimental.pallas import tpu as pltpu
from jax.sharding import PartitionSpec as P

SWEEPS = 3
f32, bf16 = jnp.float32, jnp.bfloat16
floor_term = 0.01
HBM = pl.BlockSpec(memory_space=pl.ANY)
VMEM = pl.BlockSpec(memory_space=pltpu.VMEM)


def dot(a, b):
    return jnp.dot(a, b, precision=lax.Precision.HIGHEST, preferred_element_type=f32)


def split(a):
    high = a.astype(bf16)
    return high, (a - high.astype(f32)).astype(bf16)


def paired(b):
    high, low = split(b)
    return jnp.concatenate(
        [
            jnp.concatenate([high, low], axis=1),
            jnp.concatenate([high, jnp.zeros_like(low)], axis=1),
        ],
        axis=0,
    )


def dot_paired(a, b_paired):
    both = jnp.dot(jnp.concatenate(split(a), axis=1), b_paired, preferred_element_type=f32)
    half = both.shape[1] // 2
    return both[:, :half] + both[:, half:]


def dot_three(a, b):
    return dot_paired(a, paired(b))


def rotation(block, steps=None):
    size = block.shape[0]
    row = lax.broadcasted_iota(jnp.int32, (size, size), 0)
    eye = (row == lax.broadcasted_iota(jnp.int32, (size, size), 1)).astype(f32)

    def sweep(_, carry):
        m, q = carry
        on = m * eye
        spread = jnp.sum(on, axis=0, keepdims=True) - jnp.sum(on, axis=1, keepdims=True)
        ratio = m * spread / (spread * spread + 2.0 * m * m + floor_term)
        k = 0.5 * (ratio - ratio.T)
        square = dot(k, k)
        bound = jnp.sum(jnp.abs(square), axis=0, keepdims=True)
        bound = 0.25 * 1.001 * jnp.max(bound, axis=1, keepdims=True)
        scale = 2.0 / (2.0 + bound)
        reach = bound / (2.0 + bound)
        e = eye * (1.0 - scale) + (0.25 * scale) * square
        p = 2.0 * scale * eye + scale * k

        def step(p, e, reach):
            w = 2.0 / (2.0 - reach * reach)
            both = dot_three(jnp.concatenate([p, e], axis=0), e)
            reach = reach * reach / (2.0 - reach * reach)
            return w * (p + both[:size]), eye * (1.0 - w) + w * both[size:], reach

        if steps is None:
            p, *_ = lax.while_loop(
                lambda c: c[3] > 1e-4,
                lambda c: (lambda n: (*n, jnp.max(n[2])))(step(*c[:3])),
                (p, e, reach, jnp.max(reach)),
            )
        else:
            p, *_ = lax.fori_loop(0, steps, lambda _, c: step(*c), (p, e, reach))
        rest = 2.0 * eye - p + 0.5 * dot(k, p)
        g = p + 0.5 * dot_three(p, rest) - eye
        both = dot(jnp.concatenate([m, q], axis=0), g)
        return dot(g.T, both[:size]), both[size:]

    return lax.fori_loop(0, SWEEPS, sweep, (block, eye))


def rows_at(index, span):
    return pl.ds(pl.multiple_of(index * span, span), span)


def first_kernel(
    a_ref, q_ref, qt_ref, note_ref, m_ref, send_ref, keep_ref, zero_ref,
    a_held, send_held, keep_held, zeros, w_ref, in_sem, out_sem, zero_sem,
):
    span = q_ref.shape[0]
    half = span // 2
    order = a_ref.shape[0]
    rows = zeros.shape[0]
    tiles = order // 2 // rows
    mine = rows_at(lax.axis_index("wide"), span)
    pair = pltpu.make_async_copy(a_ref.at[mine], m_ref, in_sem.at[0])
    pair.start()
    whole = pltpu.make_async_copy(a_ref, a_held, in_sem.at[1])
    whole.start()
    zeros[...] = jnp.zeros_like(zeros)
    cleared = [
        pltpu.make_async_copy(zeros, zero_ref.at[pl.ds(i * rows, rows)], zero_sem.at[i])
        for i in range(2 * tiles)
    ]
    pair.wait()
    m, q = rotation(m_ref[...])
    q_ref[...] = q
    qt = q.T
    qt_ref[...] = qt
    note_ref[:half] = qt[half:]
    note_ref[half:] = m[half:]
    m_ref[...] = m
    for copy in cleared:
        copy.start()
    w_ref[0] = paired(jnp.concatenate([q[:, half:], q[:, :half]], axis=1))
    w_ref[1] = paired(q)
    whole.wait()
    out = []
    for i in range(tiles):
        upper, lower = pl.ds(i * rows, rows), pl.ds(order // 2 + i * rows, rows)
        top = dot_paired(a_held[upper], w_ref[0])
        bottom = dot_paired(a_held[lower], w_ref[1])
        low = lax.broadcasted_iota(jnp.int32, top.shape, 1) < half
        send_held[upper] = jnp.where(low, top, bottom)
        keep_held[upper] = jnp.where(low, bottom, top)
        for n, (held, ref) in enumerate(((send_held, send_ref), (keep_held, keep_ref))):
            out.append(pltpu.make_async_copy(held.at[upper], ref.at[upper], out_sem.at[n, i]))
            out[-1].start()
    for copy in out + cleared:
        copy.wait()


def first_round(factor, rows):
    order, span = factor.shape
    square = jax.ShapeDtypeStruct((span, span), f32)
    packed = jax.ShapeDtypeStruct((order // 2, span), f32)
    tiles = order // 2 // rows
    return pl.pallas_call(
        first_kernel,
        out_shape=(
            square, square, square, square, packed, packed,
            jax.ShapeDtypeStruct((order, span), f32),
        ),
        in_specs=[HBM],
        out_specs=[VMEM] * 4 + [HBM] * 3,
        scratch_shapes=[
            pltpu.VMEM((order, span), f32),
            pltpu.VMEM((order // 2, span), f32),
            pltpu.VMEM((order // 2, span), f32),
            pltpu.VMEM((rows, span), f32),
            pltpu.VMEM((2, 2 * span, 2 * span), bf16),
            pltpu.SemaphoreType.DMA((2,)),
            pltpu.SemaphoreType.DMA((2, tiles)),
            pltpu.SemaphoreType.DMA((2 * tiles,)),
        ],
        compiler_params=pltpu.CompilerParams(vmem_limit_bytes=62 * 2**20),
        cost_estimate=pl.CostEstimate(flops=3 * 10**9, bytes_accessed=10**7, transcendentals=0),
        name="first_round",
    )(factor)


def along(axis, step):
    me = lax.axis_index("wide")
    weight = {"y": 16, "z": 4, "x": 1}[axis]
    place = lax.rem(me // weight, 4)
    return me + (lax.rem(place + step + 4, 4) - place) * weight


def remote(src, dst, sems, at, target):
    return pltpu.make_async_remote_copy(
        src_ref=src,
        dst_ref=dst,
        send_sem=sems.at[(0, *at)],
        recv_sem=sems.at[(1, *at)],
        device_id={"wide": target},
        device_id_type=pl.DeviceIdType.MESH,
    )


class Gather:
    def __init__(self, buf, ring_sems, x_sems):
        self.buf, self.ring, self.ends = buf, ring_sems, x_sems
        me = lax.axis_index("wide")
        self.y, self.z, self.x = lax.rem(me // 16, 4), lax.rem(me // 4, 4), lax.rem(me, 4)
        self.sent = []

    def start(self, src, dst, sems, at, target):
        copy = remote(src, dst, sems, at, target)
        copy.start()
        self.sent.append(copy)

    def arrived(self, place, sems, at):
        remote(place, place, sems, at, lax.axis_index("wide")).wait_recv()

    def y_start(self, src):
        place = self.buf.at[self.x, self.z, self.y]
        for i in (1, 3, 2):
            self.start(src, place, self.ring, (0, i), along("y", i))

    def y_wait(self):
        for i in (1, 3, 2):
            y = lax.rem(self.y - i + 4, 4)
            self.arrived(self.buf.at[self.x, self.z, y], self.ring, (0, i))

    def z_start(self):
        place = self.buf.at[self.x, self.z]
        for i in (1, 3, 2):
            self.start(place, place, self.ring, (1, i), along("z", i))

    def plane(self, i):
        return lax.rem(self.z - i + 4, 4)

    def z_wait(self, i):
        self.arrived(self.buf.at[self.x, self.plane(i)], self.ring, (1, i))

    def x_start(self, i):
        place = self.buf.at[self.x, self.plane(i)]
        self.start(place, place, self.ends, (0, i), along("x", 1))
        self.start(place, place, self.ends, (1, i), along("x", 3))

    def x_forward(self, i):
        for way, step in ((0, 3), (1, 1)):
            source = lax.rem(self.x + step, 4)
            place = self.buf.at[source, self.plane(i)]
            self.arrived(place, self.ends, (way, i))
            part = self.buf.at[source, self.plane(i), pl.ds(2 * way, 2)]
            self.start(part, part, self.ends, (2 + way, i), along("x", 4 - step))

    def x_wait(self, i):
        source = lax.rem(self.x + 2, 4)
        for way in (0, 1):
            part = self.buf.at[source, self.plane(i), pl.ds(2 * way, 2)]
            self.arrived(part, self.ends, (2 + way, i))

    def drain(self):
        for copy in self.sent:
            copy.wait_send()


def round_kernel(
    pieces, a_ref, q_ref, qt_ref, m_ref, note_ref, send_ref, keep_ref,
    out_ref, w_ref,
    first, second, recv, keep, z_ref, turn_pair, cross, note, turned_ref,
    local_sem, note_sem, bulk_sem, ring_one, ends_one, ring_two, ends_two,
):
    span = q_ref.shape[0]
    half = span // 2
    pairs = a_ref.shape[0] // span
    mine = lax.axis_index("wide")
    partner = along("y", 2)
    barrier = pltpu.get_barrier_semaphore()
    peers = [("y", 1), ("y", 2), ("y", 3), ("z", 1), ("z", 2), ("z", 3), ("x", 1), ("x", 3)]
    for axis, step in peers:
        pl.semaphore_signal(
            barrier, inc=1, device_id={"wide": along(axis, step)},
            device_id_type=pl.DeviceIdType.MESH,
        )
    x, z, y = lax.rem(mine, 4), lax.rem(mine // 4, 4), lax.rem(mine // 16, 4)
    local = [
        pltpu.make_async_copy(a_ref.at[rows_at(partner, span)], cross, local_sem.at[0]),
        pltpu.make_async_copy(qt_ref, first.at[x, z, y], local_sem.at[1]),
        pltpu.make_async_copy(keep_ref, keep, local_sem.at[2]),
    ]
    for copy in local:
        copy.start()
    pl.semaphore_wait(barrier, len(peers))

    told = remote(note_ref, note, note_sem, (), partner)
    told.start()
    one, two = Gather(first, ring_one, ends_one), Gather(second, ring_two, ends_two)
    one.y_start(qt_ref)
    size = send_ref.shape[0] // pieces
    bulk = [
        remote(send_ref.at[pl.ds(i * size, size)], recv.at[pl.ds(i * size, size)], bulk_sem, (i,), partner)
        for i in range(pieces)
    ]
    early = pieces // 2
    for copy in bulk[:early]:
        copy.start()
    local[1].wait()
    one.y_wait()
    one.z_start()
    one.x_start(0)

    local[0].wait()
    told.wait_recv()
    q = q_ref[...]
    across = dot(note[:half], dot(cross[...], q))[:, :half]
    m = m_ref[...]
    block = jnp.concatenate(
        [
            jnp.concatenate([m[:half, :half], across.T], axis=1),
            jnp.concatenate([across, note[half:, half:]], axis=1),
        ],
        axis=0,
    )
    _, turn = rotation(block, 8)
    turned = turn.T
    turned_ref[...] = turned
    w_ref[0] = dot(qt_ref[:half].T, turn[:half])
    w_ref[1] = dot(note[:half].T, turn[half:])
    turn_pair[0] = paired(jnp.concatenate([turn[half:], turn[:half]], axis=0))
    turn_pair[1] = paired(turn)
    second[x, z, y] = turned
    two.y_start(turned_ref)
    for copy in bulk[early:]:
        copy.start()
    for i in (1, 3, 2):
        one.z_wait(i)
        one.x_start(i)
    one.x_forward(0)
    two.y_wait()
    two.z_start()
    for i in (1, 3, 2):
        one.x_forward(i)
    two.x_start(0)
    for i in (1, 3, 2):
        two.z_wait(i)
        two.x_start(i)
    for i in (0, 1, 3, 2):
        one.x_wait(i)

    local[2].wait()
    for copy in bulk:
        copy.wait_recv()
    low = lax.broadcasted_iota(jnp.int32, (span, span), 1) < half

    def near(n, carry):
        at = rows_at(n, span)
        got, held = recv[at], keep[at]
        place = (lax.rem(n, 4), lax.rem(n // 4, 4))
        top = dot_paired(jnp.where(low, got, held), turn_pair[0])
        bottom = dot_paired(jnp.where(low, held, got), turn_pair[1])
        upper = dot_three(first[(*place, n // 16)], top)
        lower = dot_three(first[(*place, n // 16 + 2)], bottom)
        z_ref[0, at] = jnp.concatenate([upper[:half], lower[half:]], axis=0)
        z_ref[1, at] = jnp.concatenate([lower[:half], upper[half:]], axis=0)
        return carry

    lax.fori_loop(0, pairs // 2, near, 0)

    def far(x_at, z_at):
        for b in range(2):
            at = rows_at(16 * b + 4 * z_at + x_at, span)
            for side in range(2):
                out_ref[side, at] = dot_three(second[x_at, z_at, b + 2 * side], z_ref[side, at])

    for i in (0, 1, 3, 2):
        two.x_forward(i)
        for step in (0, 1, 3):
            far(lax.rem(x + step, 4), two.plane(i))
    for i in (0, 1, 3, 2):
        two.x_wait(i)
        far(lax.rem(x + 2, 4), two.plane(i))
    told.wait_send()
    for copy in bulk:
        copy.wait_send()
    one.drain()
    two.drain()


def rounds(factor, q, qt, m, note, send, keep, pieces):
    order, span = factor.shape
    gathered = pltpu.VMEM((4, 4, 4, span, span), f32)
    packed = pltpu.VMEM((order // 2, span), f32)
    square = pltpu.VMEM((span, span), f32)
    ring, ends = pltpu.SemaphoreType.DMA((2, 2, 4)), pltpu.SemaphoreType.DMA((2, 4, 4))
    return pl.pallas_call(
        functools.partial(round_kernel, pieces),
        out_shape=(
            jax.ShapeDtypeStruct((2, order // 2, span), f32),
            jax.ShapeDtypeStruct((2, span, span), f32),
        ),
        in_specs=[HBM, VMEM, VMEM, VMEM, VMEM, HBM, HBM],
        out_specs=[VMEM, VMEM],
        scratch_shapes=[
            gathered, gathered, packed, packed,
            pltpu.VMEM((2, order // 2, span), f32),
            pltpu.VMEM((2, 2 * span, 2 * span), bf16),
            square, square, square,
            pltpu.SemaphoreType.DMA((3,)),
            pltpu.SemaphoreType.DMA((2,)),
            pltpu.SemaphoreType.DMA((2, pieces)),
            ring, ends, ring, ends,
        ],
        compiler_params=pltpu.CompilerParams(
            collective_id=0, has_side_effects=True, vmem_limit_bytes=62 * 2**20
        ),
        cost_estimate=pl.CostEstimate(flops=10**10, bytes_accessed=10**7, transcendentals=0),
        name="rounds",
    )(factor, q, qt, m, note, send, keep)


def body(pairs, factor):
    order, span = factor.shape
    mine = lax.axis_index("wide")
    other = lax.rem(mine + pairs // 2, pairs)
    q, qt, note, m, send, keep, basis = first_round(factor, 512)
    rotated, w = rounds(factor, q, qt, m, note, send, keep, 8)
    basis = lax.dynamic_update_slice_in_dim(basis, w[0], mine * span, 0)
    basis = lax.dynamic_update_slice_in_dim(basis, w[1], other * span, 0)
    return rotated.reshape(order, span), basis


def solution(mesh):
    spec = P("layer", "wide")
    return jax.shard_map(
        functools.partial(body, mesh.shape["wide"]),
        mesh=mesh,
        in_specs=(spec,),
        out_specs=(spec, spec),
        check_vma=False,
    )
```

time: 427 us -> 112 us (0.26)
  waiting for transfers between devices: 360 us -> 0 us
  Pallas kernels: 40.6 us -> 102 us
  between operations: 14.1 us -> 0.65 us
  starting transfers between devices: 6.59 us -> 0 us
    all_gather x1 -> x0, waiting for transfers between devices: 316 us -> none  [body(): rotated = last_step(recv, keep, turn, lax.all_gather(wt, 'wide'), 2)]
    pallas_call x3 -> x2, Pallas kernels: 40.6 us -> 102 us  [the longest x1 91.3 us: rounds(): pl.pallas_call(functools.partial(round_kernel, pieces), out_shape=(jax.Sh...]
    ppermute x2 -> x0, waiting for transfers between devices: 44 us -> none  [the longest x1 41.2 us: body(): recv = lax.ppermute(send, 'wide', partners)]
    ppermute x2 -> x0, starting transfers between devices: 6.55 us -> none  [the longest x1 3.27 us: body(): note = lax.ppermute(note, 'wide', partners)]
  transfers between devices with their start and end apart: 3 -> 0, of which waited for: 3 -> 0; matrix products, arithmetic and copies ran while one was open for 1% -> 0% of each run, Pallas kernels for 0% -> 0%
where the time goes in v2:
time: 112 us; the launch traced here: 110 us
  Pallas kernels  102 us (91%)
  local copies, waits for them, and re-layouts  7.42 us (7%)
    pallas_call x1, Pallas kernels, rounds(): pl.pallas_call(functools.partial(round_kernel, pieces), out_shape=(jax.Sh...  91.3 us
    pallas_call x1, Pallas kernels, first_round(): pl.pallas_call(first_kernel, out_shape=(square, square, square, square, p...  10.6 us
    unnamed x1, local copies, waits for them, and re-layouts  4.47 us

profile of v2, /device:TPU:2, one launch (start us, length us, event | category | flops | bytes accessed | tf_op | source)
XLA Modules:
  0.0 110.0 jit_solution(4550393433652013658)
XLA Ops:
  0.6 10.6 %first_round.1 = (f32[128,128]{1,0:T(8,128)}, f32[128,128]{1,0:T(8,128)}, f32[128,128]{1,0:T(8,128)}, f32[128,128]{1,0:T(8,128)}, f32[4096,128]{1,0:T(8,128)}, /*index=5*/f32[4096,128]{1,0:T(8,128)}, f32[8192,128]{1,0:T(8,128)}) custom-call(f32[8192,128]{1,0:T(8,128)} %a_ref.3), custom_call_target="tpu_custom_call" | custom-call | flops 3000000000 | bytes 10000000 | tf_op jit(solution)/shard_map/first_round/pallas_call | solution.py:144
  11.3 91.3 %rounds.1 = (f32[2,4096,128]{2,1,0:T(8,128)}, f32[2,128,128]{2,1,0:T(8,128)}) custom-call(f32[8192,128]{1,0:T(8,128)} %a_ref.3, f32[128,128]{1,0:T(8,128)} %get-tuple-element.11.q_ref, f32[128,128]{1,0:T(8,128)} %get-tuple-element.12.qt_ref, f32[128,128]{1,0:T(8,128)} %get-tuple-element.13.m_ref, f32[128,128]{1,0:T(8,128)} %get-tuple-element.14.note_ref, ...), custom_call_target="tpu_custom_call" | custom-call | flops 10000000000 | bytes 10000000 | tf_op jit(solution)/shard_map/rounds/pallas_call | solution.py:374
  102.6 1.5 %bitcast_dynamic-update-slice_fusion.1 = f32[8192,128]{1,0:T(8,128)} fusion(f32[8192,128]{1,0:T(8,128)} %get-tuple-element.18, s32[]{:T(128)S(6)} %select_n.6, f32[2,128,128]{2,1,0:T(8,128)} %get-tuple-element.19), kind=kLoop, calls=%fused_computation.1 | loop fusion | bytes 131076 | tf_op jit(solution)/shard_map/dynamic_update_slice | solution.py:406
  104.1 1.5 %bitcast_dynamic-update-slice_fusion = f32[8192,128]{1,0:T(8,128)} fusion(f32[8192,128]{1,0:T(8,128)} %bitcast_dynamic-update-slice_fusion.1, s32[]{:T(128)S(6)} %select_n.7, f32[2,128,128]{2,1,0:T(8,128)} %get-tuple-element.19), kind=kLoop, calls=%fused_computation | loop fusion | bytes 131076 | tf_op jit(solution)/shard_map/dynamic_update_slice | solution.py:407
  105.6 4.5 %copy.6 = f32[8192,128]{1,0:T(8,128)} copy(f32[8192,128]{1,0:T(8,128)} %bitcast.5) | data formatting | bytes 8388608

commit v3 on v2

v3 whole, which is shorter than its diff:
```python
import jax
import jax.numpy as jnp
from jax import lax
from jax.experimental import pallas as pl
from jax.experimental.pallas import tpu as pltpu
from jax.sharding import PartitionSpec as P

SWEEPS = 3
f32, bf16 = jnp.float32, jnp.bfloat16
floor_term = 0.01
HBM = pl.BlockSpec(memory_space=pl.ANY)
VMEM = pl.BlockSpec(memory_space=pltpu.VMEM)


def dot(a, b):
    return jnp.dot(a, b, precision=lax.Precision.HIGHEST, preferred_element_type=f32)


def split(a):
    high = a.astype(bf16)
    return high, (a - high.astype(f32)).astype(bf16)


def paired(b):
    high, low = split(b)
    return jnp.concatenate(
        [
            jnp.concatenate([high, low], axis=1),
            jnp.concatenate([high, jnp.zeros_like(low)], axis=1),
        ],
        axis=0,
    )


def dot_paired(a, b_paired):
    both = jnp.dot(jnp.concatenate(split(a), axis=1), b_paired, preferred_element_type=f32)
    half = both.shape[1] // 2
    return both[:, :half] + both[:, half:]


def dot_three(a, b):
    return dot_paired(a, paired(b))


def rotation(block, steps=None, between=None):
    size = block.shape[0]
    row = lax.broadcasted_iota(jnp.int32, (size, size), 0)
    eye = (row == lax.broadcasted_iota(jnp.int32, (size, size), 1)).astype(f32)

    def sweep(_, carry):
        m, q = carry
        on = m * eye
        spread = jnp.sum(on, axis=0, keepdims=True) - jnp.sum(on, axis=1, keepdims=True)
        ratio = m * spread / (spread * spread + 2.0 * m * m + floor_term)
        k = 0.5 * (ratio - ratio.T)
        square = dot(k, k)
        bound = jnp.sum(jnp.abs(square), axis=0, keepdims=True)
        bound = 0.25 * 1.001 * jnp.max(bound, axis=1, keepdims=True)
        scale = 2.0 / (2.0 + bound)
        reach = bound / (2.0 + bound)
        e = eye * (1.0 - scale) + (0.25 * scale) * square
        p = 2.0 * scale * eye + scale * k

        def step(p, e, reach):
            w = 2.0 / (2.0 - reach * reach)
            both = dot_three(jnp.concatenate([p, e], axis=0), e)
            reach = reach * reach / (2.0 - reach * reach)
            return w * (p + both[:size]), eye * (1.0 - w) + w * both[size:], reach

        if steps is None:
            p, *_ = lax.while_loop(
                lambda c: c[3] > 1e-4,
                lambda c: (lambda n: (*n, jnp.max(n[2])))(step(*c[:3])),
                (p, e, reach, jnp.max(reach)),
            )
        else:
            p, *_ = lax.fori_loop(0, steps, lambda _, c: step(*c), (p, e, reach))
        rest = 2.0 * eye - p + 0.5 * dot(k, p)
        g = p + 0.5 * dot_three(p, rest) - eye
        both = dot(jnp.concatenate([m, q], axis=0), g)
        return dot(g.T, both[:size]), both[size:]

    if between is None:
        return lax.fori_loop(0, SWEEPS, sweep, (block, eye))
    carry = (block, eye)
    for repeat in range(SWEEPS):
        carry = sweep(repeat, carry)
        between(repeat)
    return carry


def rows_at(index, span):
    return pl.ds(pl.multiple_of(index * span, span), span)


def first_kernel(a_ref, q_ref, qt_ref, note_ref, m_ref, zero_ref, zeros, in_sem, zero_sem):
    span = q_ref.shape[0]
    half = span // 2
    rows = zeros.shape[0]
    mine = rows_at(lax.axis_index("wide"), span)
    pair = pltpu.make_async_copy(a_ref.at[mine], m_ref, in_sem)
    pair.start()
    zeros[...] = jnp.zeros_like(zeros)
    cleared = [
        pltpu.make_async_copy(zeros, zero_ref.at[pl.ds(i * rows, rows)], zero_sem.at[i])
        for i in range(zero_ref.shape[0] // rows)
    ]
    pair.wait()
    for copy in cleared:
        copy.start()
    m, q = rotation(m_ref[...])
    q_ref[...] = q
    qt = q.T
    qt_ref[...] = qt
    note_ref[:half] = qt[half:]
    note_ref[half:] = m[half:]
    m_ref[...] = m
    for copy in cleared:
        copy.wait()


def first_round(factor, rows):
    order, span = factor.shape
    square = jax.ShapeDtypeStruct((span, span), f32)
    return pl.pallas_call(
        first_kernel,
        out_shape=(square, square, square, square, jax.ShapeDtypeStruct((order, span), f32)),
        in_specs=[HBM],
        out_specs=[VMEM] * 4 + [HBM],
        scratch_shapes=[
            pltpu.VMEM((rows, span), f32),
            pltpu.SemaphoreType.DMA,
            pltpu.SemaphoreType.DMA((order // rows,)),
        ],
        compiler_params=pltpu.CompilerParams(vmem_limit_bytes=62 * 2**20),
        cost_estimate=pl.CostEstimate(flops=10**9, bytes_accessed=10**7, transcendentals=0),
        name="first_round",
    )(factor)


WEIGHT = {"y": 16, "z": 4, "x": 1}


def along(axis, step):
    me = lax.axis_index("wide")
    place = lax.rem(me // WEIGHT[axis], 4)
    return me + (lax.rem(place + step + 4, 4) - place) * WEIGHT[axis]


def remote(src, dst, send_sem, recv_sem, target):
    return pltpu.make_async_remote_copy(
        src_ref=src,
        dst_ref=dst,
        send_sem=send_sem,
        recv_sem=recv_sem,
        device_id={"wide": target},
        device_id_type=pl.DeviceIdType.MESH,
    )


class Gather:
    def __init__(self, buf, y_sems, z_send, z_recv, x_sems):
        self.buf, self.y_sems, self.x_sems = buf, y_sems, x_sems
        self.z_send, self.z_recv = z_send, z_recv
        self.me = lax.axis_index("wide")
        self.y, self.z, self.x = (lax.rem(self.me // WEIGHT[a], 4) for a in "yzx")
        self.sent, self.sent_if = [], []

    def start(self, src, dst, sems, at, target):
        copy = remote(src, dst, sems.at[(0, *at)], sems.at[(1, *at)], target)
        copy.start()
        self.sent.append(copy)

    def arrived(self, place, recv_sem):
        remote(place, place, recv_sem, recv_sem, self.me).wait_recv()

    def y_start(self, src):
        place = self.at(self.x, self.z, self.y)
        for i in (1, 3, 2):
            self.start(src, place, self.y_sems, (i,), along("y", i))

    def y_wait(self):
        for i in (1, 3, 2):
            y = lax.rem(self.y - i + 4, 4)
            self.arrived(self.at(self.x, self.z, y), self.y_sems.at[1, i])

    def plane(self, r):
        far = self.z // 2
        return (self.z, self.z + 1 - 2 * lax.rem(self.z, 2), 2 - far, 3 - 3 * far)[r]

    def z_move(self, condition, plane, slot, to):
        place = self.z_block(plane)
        target = self.me + (to - self.z) * WEIGHT["z"]
        copy = remote(place, place, self.z_send.at[slot], self.z_recv.at[plane], target)
        pl.when(condition)(copy.start)
        self.sent_if.append((condition, copy))

    def z_start(self):
        self.z_move(self.z < 3, self.z, 0, lax.rem(self.z + 1, 4))
        self.z_move(self.z > 0, self.z, 1, lax.rem(self.z + 3, 4))

    def z_take(self, r):
        plane = self.plane(r)
        self.arrived(self.z_block(plane), self.z_recv.at[plane])
        inner = lax.rem(self.z + 1, 4) // 2 == 1
        to = 3 - self.z if r == 1 else 3 * lax.rem(self.z + 3, 4)
        self.z_move(inner, plane, 1 + r, lax.rem(to, 4))

    def x_start(self, r):
        for way, step in ((0, 1), (1, 3)):
            for turn in range(2):
                part = self.at(self.x, self.plane(r), pl.ds(2 * ((way + turn) % 2), 2))
                self.start(part, part, self.x_sems, (2 * way + turn, r), along("x", step))

    def x_forward(self, r):
        for way, step in ((0, 3), (1, 1)):
            part = self.at(lax.rem(self.x + step, 4), self.plane(r), pl.ds(2 * way, 2))
            self.arrived(part, self.x_sems.at[1, 2 * way, r])
            self.start(part, part, self.x_sems, (4 + way, r), along("x", 4 - step))

    def x_near(self, r):
        for way, step in ((0, 3), (1, 1)):
            part = self.at(lax.rem(self.x + step, 4), self.plane(r), pl.ds(2 - 2 * way, 2))
            self.arrived(part, self.x_sems.at[1, 2 * way + 1, r])

    def x_far(self, r):
        for way in (0, 1):
            part = self.at(lax.rem(self.x + 2, 4), self.plane(r), pl.ds(2 * way, 2))
            self.arrived(part, self.x_sems.at[1, 4 + way, r])

    def drain(self):
        for copy in self.sent:
            copy.wait_send()
        for condition, copy in self.sent_if:
            pl.when(condition)(copy.wait_send)
        self.sent, self.sent_if = [], []


class RingLast(Gather):
    def at(self, x, z, *y):
        return self.buf.at[(x, z, *y)]

    def z_block(self, z):
        return self.buf.at[self.x, z]


class LineLast(Gather):
    def at(self, x, z, *y):
        return self.buf.at[(z, x, *y)]

    def z_block(self, z):
        return self.buf.at[z]


GATHER_SEMS = [
    pltpu.SemaphoreType.DMA((2, 4)),
    pltpu.SemaphoreType.DMA((5,)),
    pltpu.SemaphoreType.DMA((4,)),
    pltpu.SemaphoreType.DMA((2, 6, 4)),
]


def round_kernel(
    a_ref, q_ref, qt_ref, m_ref, note_ref,
    out_ref, w_ref,
    first, second, third, held, send, recv, keep, z_ref, q_pair, turn_pair, note, upper_ref, lower_ref,
    local_sem, note_sem, bulk_sem, *gather_sems,
):
    span = q_ref.shape[0]
    half = span // 2
    cut = upper_ref.shape[0]
    order = a_ref.shape[0]
    pairs = order // span
    partner = along("y", 2)
    barrier = pltpu.get_barrier_semaphore()
    peers = [("y", 1), ("y", 2), ("y", 3), ("z", 1), ("z", 3), ("x", 1), ("x", 3)]
    for axis, step in peers:
        pl.semaphore_signal(
            barrier, inc=1, device_id={"wide": along(axis, step)},
            device_id_type=pl.DeviceIdType.MESH,
        )
    one = RingLast(first, *gather_sems[:4])
    two = RingLast(second, *gather_sems[4:8])
    three = LineLast(third, *gather_sems[8:])
    x, z, y = one.x, one.z, one.y
    mine = pltpu.make_async_copy(qt_ref, first.at[x, z, y], local_sem.at[0])
    mine.start()
    whole = pltpu.make_async_copy(a_ref, held, local_sem.at[1])
    whole.start()
    q = q_ref[...]
    q_pair[0] = paired(jnp.concatenate([q[:, half:], q[:, :half]], axis=1))
    q_pair[1] = paired(q)
    pl.semaphore_wait(barrier, len(peers))
    told = remote(note_ref, note, note_sem.at[0], note_sem.at[1], partner)
    told.start()
    one.y_start(qt_ref)

    whole.wait()
    size = 4 * span
    low = lax.broadcasted_iota(jnp.int32, (size, span), 1) < half

    def halves(i, carry):
        at = rows_at(i, size)
        top = dot_paired(held[at], q_pair[0])
        bottom = dot_paired(held[rows_at(i + pairs // 8, size)], q_pair[1])
        send[at] = jnp.where(low, top, bottom)
        keep[at] = jnp.where(low, bottom, top)
        return carry

    lax.fori_loop(0, pairs // 8, halves, 0)
    across = dot(held[rows_at(partner, span)], q)
    bulk = []
    for r in range(4):
        for b in range(2):
            at = rows_at(4 * b + one.plane(r), size)
            sems = (bulk_sem.at[0, r, b], bulk_sem.at[1, r, b])
            bulk.append(remote(send.at[at], recv.at[at], *sems, partner))
    for copy in bulk[:2]:
        copy.start()
    told.wait_recv()
    across = dot(note[:half], across)[:, :half]
    m = m_ref[...]
    block = jnp.concatenate(
        [
            jnp.concatenate([m[:half, :half], across.T], axis=1),
            jnp.concatenate([across, note[half:, half:]], axis=1),
        ],
        axis=0,
    )
    mine.wait()
    one.y_wait()
    one.z_start()
    one.x_start(0)

    def between(repeat):
        if repeat == 1:
            one.x_forward(0)
        if repeat == 2:
            one.z_take(1)
            one.x_start(1)

    _, turn = rotation(block, 7, between)
    turned = turn.T
    upper_ref[...] = turned[:cut]
    lower_ref[...] = turned[cut:]
    second[x, z, y] = turned[:cut]
    third[z, x, y] = turned[cut:]
    turn_pair[0] = paired(jnp.concatenate([turn[half:], turn[:half]], axis=0))
    turn_pair[1] = paired(turn)
    three.y_start(lower_ref)
    two.y_start(upper_ref)
    w_ref[0] = dot(qt_ref[:half].T, turn[:half])
    w_ref[1] = dot(note[:half].T, turn[half:])
    low = low[:span]

    def near(r):
        for copy in bulk[2 * r : 2 * r + 2]:
            copy.wait_recv()
        z_at = one.plane(r)

        def each(t, carry):
            n = 16 * (t // 4) + 4 * z_at + lax.rem(t, 4)
            at = rows_at(n, span)
            got, kept = recv[at], keep[at]
            group = first.at[lax.rem(t, 4), z_at]
            top = dot_paired(jnp.where(low, got, kept), turn_pair[0])
            bottom = dot_paired(jnp.where(low, kept, got), turn_pair[1])
            upper = dot_three(group[t // 4], top)
            lower = dot_three(group[t // 4 + 2], bottom)
            z_ref[0, n] = paired(jnp.concatenate([upper[:half], lower[half:]], axis=0))
            z_ref[1, n] = paired(jnp.concatenate([lower[:half], upper[half:]], axis=0))
            return carry

        lax.fori_loop(0, 8, each, 0)

    def far(group, start, count, x_at, z_at):
        for b in range(2):
            n = 16 * b + 4 * z_at + x_at
            at = pl.ds(pl.multiple_of(n * span, span) + start, count)
            for side in range(2):
                out_ref[side, at] = dot_paired(group[b + 2 * side], z_ref[side, n])

    def far_ring(r, steps):
        for step in steps:
            x_at, z_at = lax.rem(x + step, 4), two.plane(r)
            far(second.at[x_at, z_at], 0, cut, x_at, z_at)

    def far_line(r):
        for step in range(4):
            x_at, z_at = lax.rem(x + step, 4), three.plane(r)
            far(third.at[z_at, x_at], cut, span - cut, x_at, z_at)

    three.drain()
    two.drain()
    for copy in bulk[2:]:
        copy.start()
    three.y_wait()
    three.x_start(0)
    two.y_wait()
    two.z_start()
    one.x_forward(1)
    one.z_take(2)
    one.x_start(2)
    one.x_near(0)
    one.x_far(0)
    near(0)
    three.x_forward(0)
    two.x_start(0)
    one.z_take(3)
    one.x_start(3)
    one.x_forward(2)
    three.x_near(0)
    three.x_far(0)
    three.z_start()
    two.z_take(1)
    two.x_start(1)
    two.x_forward(0)
    one.x_near(1)
    one.x_far(1)
    near(1)
    two.z_take(2)
    two.x_start(2)
    one.x_forward(3)
    three.z_take(1)
    one.x_near(2)
    one.x_far(2)
    near(2)
    two.z_take(3)
    two.x_start(3)
    two.x_forward(1)
    three.z_take(2)
    one.x_near(3)
    one.x_far(3)
    near(3)
    two.x_forward(2)
    far_line(0)
    far_ring(0, (0,))
    two.x_near(0)
    far_ring(0, (1, 3))
    three.z_take(3)
    two.x_forward(3)
    two.x_far(0)
    far_ring(0, (2,))
    for r in (1, 2):
        far_line(r)
        two.x_near(r)
        two.x_far(r)
        far_ring(r, range(4))
    far_line(3)
    two.x_near(3)
    far_ring(3, (0, 1, 3))
    two.x_far(3)
    far_ring(3, (2,))
    told.wait_send()
    for copy in bulk:
        copy.wait_send()
    for gather in (one, two, three):
        gather.drain()


def rounds(factor, q, qt, m, note, cut):
    order, span = factor.shape
    packed = pltpu.VMEM((order // 2, span), f32)
    square = pltpu.VMEM((span, span), f32)
    pair = pltpu.VMEM((2, 2 * span, 2 * span), bf16)
    return pl.pallas_call(
        round_kernel,
        out_shape=(
            jax.ShapeDtypeStruct((2, order // 2, span), f32),
            jax.ShapeDtypeStruct((2, span, span), f32),
        ),
        in_specs=[HBM, VMEM, VMEM, VMEM, VMEM],
        out_specs=[VMEM, VMEM],
        scratch_shapes=[
            pltpu.VMEM((4, 4, 4, span, span), f32),
            pltpu.VMEM((4, 4, 4, cut, span), f32),
            pltpu.VMEM((4, 4, 4, span - cut, span), f32),
            pltpu.VMEM((order, span), f32),
            packed, packed, packed,
            pltpu.VMEM((2, order // span // 2, 2 * span, 2 * span), bf16),
            pair, pair, square,
            pltpu.VMEM((cut, span), f32),
            pltpu.VMEM((span - cut, span), f32),
            pltpu.SemaphoreType.DMA((2,)),
            pltpu.SemaphoreType.DMA((2,)),
            pltpu.SemaphoreType.DMA((2, 4, 2)),
            *(GATHER_SEMS * 3),
        ],
        compiler_params=pltpu.CompilerParams(
            collective_id=0, has_side_effects=True, vmem_limit_bytes=62 * 2**20
        ),
        cost_estimate=pl.CostEstimate(flops=10**10, bytes_accessed=10**7, transcendentals=0),
        name="rounds",
    )(factor, q, qt, m, note)


def finish_kernel(rotated_ref, w_ref, zero_ref, out_ref, basis_ref, held, in_sem, out_sem, w_sem):
    del zero_ref
    pairs = basis_ref.shape[0] // w_ref.shape[1]
    mine = lax.axis_index("wide")
    places = (mine, lax.rem(mine + pairs // 2, pairs))
    tiles = in_sem.shape[0]
    rows = held.shape[0] // tiles
    parts = [pl.ds(i * rows, rows) for i in range(tiles)]
    taken = [
        pltpu.make_async_copy(rotated_ref.at[p], held.at[p], in_sem.at[i])
        for i, p in enumerate(parts)
    ]
    put = [
        pltpu.make_async_copy(held.at[p], out_ref.at[p], out_sem.at[i])
        for i, p in enumerate(parts)
    ]
    for copy in taken:
        copy.start()
    blocks = [
        pltpu.make_async_copy(w_ref.at[i], basis_ref.at[rows_at(p, w_ref.shape[1])], w_sem.at[i])
        for i, p in enumerate(places)
    ]
    for copy in blocks:
        copy.start()
    for got, sent in zip(taken, put):
        got.wait()
        sent.start()
    for copy in put + blocks:
        copy.wait()


def finish(rotated, w, basis, tiles):
    order, span = basis.shape
    shape = jax.ShapeDtypeStruct((order, span), f32)
    return pl.pallas_call(
        finish_kernel,
        out_shape=(shape, shape),
        in_specs=[HBM, VMEM, HBM],
        out_specs=[HBM, HBM],
        input_output_aliases={2: 1},
        scratch_shapes=[
            pltpu.VMEM((order, span), f32),
            pltpu.SemaphoreType.DMA((tiles,)),
            pltpu.SemaphoreType.DMA((tiles,)),
            pltpu.SemaphoreType.DMA((2,)),
        ],
        compiler_params=pltpu.CompilerParams(vmem_limit_bytes=62 * 2**20),
        cost_estimate=pl.CostEstimate(flops=10**6, bytes_accessed=10**7, transcendentals=0),
        name="finish",
    )(rotated, w, basis)


def body(factor):
    q, qt, note, m, basis = first_round(factor, 512)
    rotated, w = rounds(factor, q, qt, m, note, 88)
    return finish(rotated.reshape(factor.shape), w, basis, 8)


def solution(mesh):
    spec = P("layer", "wide")
    return jax.shard_map(
        body,
        mesh=mesh,
        in_specs=(spec,),
        out_specs=(spec, spec),
        check_vma=False,
    )
```

time: 112 us -> 120 us (1.071)
  Pallas kernels: 102 us -> 118 us
  local copies, waits for them, and re-layouts: 7.42 us -> 0 us
    pallas_call x2 -> x3, Pallas kernels: 102 us -> 118 us  [the longest x1 105 us: rounds(): pl.pallas_call(round_kernel, out_shape=(jax.ShapeDtypeStruct((2, order //...]
    unnamed x1 -> x0, local copies, waits for them, and re-layouts: 4.47 us -> none
    dynamic_update_slice x2 -> x0, local copies, waits for them, and re-layouts: 2.95 us -> none  [the longest x1 1.48 us: body(): basis = lax.dynamic_update_slice_in_dim(basis, w[0], mine * span, 0)]
where the time goes in v3:
time: 120 us; the launch traced here: 118 us
  Pallas kernels  118 us (98%)
    pallas_call x1, Pallas kernels, rounds(): pl.pallas_call(round_kernel, out_shape=(jax.ShapeDtypeStruct((2, order //...  105 us
    pallas_call x1, Pallas kernels, first_round(): pl.pallas_call(first_kernel, out_shape=(square, square, square, square, j...  8.21 us
    pallas_call x1, Pallas kernels, finish(): pl.pallas_call(finish_kernel, out_shape=(shape, shape), in_specs=[HBM, VM...  4.55 us

profile of v3, /device:TPU:2, one launch (start us, length us, event | category | flops | bytes accessed | tf_op | source)
XLA Modules:
  0.0 118.3 jit_solution(13382132503117118064)
XLA Ops:
  0.6 8.2 %first_round.1 = (f32[128,128]{1,0:T(8,128)}, f32[128,128]{1,0:T(8,128)}, f32[128,128]{1,0:T(8,128)}, f32[128,128]{1,0:T(8,128)}, f32[8192,128]{1,0:T(8,128)}) custom-call(f32[8192,128]{1,0:T(8,128)} %a_ref.3), custom_call_target="tpu_custom_call" | custom-call | flops 1000000000 | bytes 10000000 | tf_op jit(solution)/shard_map/first_round/pallas_call | solution.py:125
  8.8 104.9 %rounds.1 = (f32[2,4096,128]{2,1,0:T(8,128)}, f32[2,128,128]{2,1,0:T(8,128)}) custom-call(f32[8192,128]{1,0:T(8,128)} %a_ref.3, f32[128,128]{1,0:T(8,128)} %get-tuple-element.9.q_ref, f32[128,128]{1,0:T(8,128)} %get-tuple-element.10.qt_ref, f32[128,128]{1,0:T(8,128)} %get-tuple-element.11.m_ref, f32[128,128]{1,0:T(8,128)} %get-tuple-element.12.note_ref), custom_call_target="tpu_custom_call" | custom-call | flops 10000000000 | bytes 10000000 | tf_op jit(solution)/shard_map/rounds/pallas_call | solution.py:466
  113.7 4.5 %finish.1 = (f32[8192,128]{1,0:T(8,128)}, f32[8192,128]{1,0:T(8,128)}) custom-call(f32[8192,128]{1,0:T(8,128)} %bitcast.1, f32[2,128,128]{2,1,0:T(8,128)} %get-tuple-element.14.w_ref, f32[8192,128]{1,0:T(8,128)} %get-tuple-element.15.zero_ref), custom_call_target="tpu_custom_call", output_to_operand_aliasing={{1}: (2, {})} | custom-call | flops 1000000 | bytes 10000000 | tf_op jit(solution)/shard_map/finish/pallas_call | solution.py:531

commit v4 on v3

--- a/solution.py
+++ b/solution.py
@@ -200,11 +200,20 @@
         self.z_move(self.z > 0, self.z, 1, lax.rem(self.z + 3, 4))
 
     def z_take(self, r):
+        self.z_relay(r)
+        self.z_end(r)
+
+    def z_relay(self, r):
         plane = self.plane(r)
-        self.arrived(self.z_block(plane), self.z_recv.at[plane])
         inner = lax.rem(self.z + 1, 4) // 2 == 1
+        pl.when(inner)(lambda: self.arrived(self.z_block(plane), self.z_recv.at[plane]))
         to = 3 - self.z if r == 1 else 3 * lax.rem(self.z + 3, 4)
         self.z_move(inner, plane, 1 + r, lax.rem(to, 4))
+
+    def z_end(self, r):
+        plane = self.plane(r)
+        end = lax.rem(self.z + 1, 4) // 2 == 0
+        pl.when(end)(lambda: self.arrived(self.z_block(plane), self.z_recv.at[plane]))
 
     def x_start(self, r):
         for way, step in ((0, 1), (1, 3)):
@@ -264,7 +273,7 @@
     a_ref, q_ref, qt_ref, m_ref, note_ref,
     out_ref, w_ref,
     first, second, third, held, send, recv, keep, z_ref, q_pair, turn_pair, note, upper_ref, lower_ref,
-    local_sem, note_sem, bulk_sem, *gather_sems,
+    local_sem, note_sem, bulk_sem, ready_sem, *gather_sems,
 ):
     span = q_ref.shape[0]
     half = span // 2
@@ -392,21 +401,28 @@
 
     three.drain()
     two.drain()
-    for copy in bulk[2:]:
-        copy.start()
     three.y_wait()
+    two.y_wait()
+    for step in (1, 2, 3):
+        pl.semaphore_signal(
+            ready_sem, inc=1, device_id={"wide": along("y", step)},
+            device_id_type=pl.DeviceIdType.MESH,
+        )
     three.x_start(0)
-    two.y_wait()
     two.z_start()
     one.x_forward(1)
     one.z_take(2)
     one.x_start(2)
+    one.z_relay(3)
+    pl.semaphore_wait(ready_sem, 3)
+    for copy in bulk[2:]:
+        copy.start()
     one.x_near(0)
     one.x_far(0)
     near(0)
     three.x_forward(0)
     two.x_start(0)
-    one.z_take(3)
+    one.z_end(3)
     one.x_start(3)
     one.x_forward(2)
     three.x_near(0)
@@ -414,30 +430,33 @@
     three.z_start()
     two.z_take(1)
     two.x_start(1)
+    two.z_relay(2)
     two.x_forward(0)
     one.x_near(1)
     one.x_far(1)
     near(1)
-    two.z_take(2)
+    two.z_end(2)
     two.x_start(2)
+    two.z_relay(3)
+    three.z_take(1)
+    three.z_relay(2)
     one.x_forward(3)
-    three.z_take(1)
     one.x_near(2)
     one.x_far(2)
     near(2)
-    two.z_take(3)
+    two.z_end(3)
     two.x_start(3)
     two.x_forward(1)
-    three.z_take(2)
     one.x_near(3)
     one.x_far(3)
+    three.z_relay(3)
     near(3)
+    three.z_end(2)
     two.x_forward(2)
     far_line(0)
     far_ring(0, (0,))
     two.x_near(0)
     far_ring(0, (1, 3))
-    three.z_take(3)
     two.x_forward(3)
     two.x_far(0)
     far_ring(0, (2,))
@@ -446,9 +465,10 @@
         two.x_near(r)
         two.x_far(r)
         far_ring(r, range(4))
-    far_line(3)
     two.x_near(3)
     far_ring(3, (0, 1, 3))
+    three.z_end(3)
+    far_line(3)
     two.x_far(3)
     far_ring(3, (2,))
     told.wait_send()
@@ -484,6 +504,7 @@
             pltpu.SemaphoreType.DMA((2,)),
             pltpu.SemaphoreType.DMA((2,)),
             pltpu.SemaphoreType.DMA((2, 4, 2)),
+            pltpu.SemaphoreType.REGULAR,
             *(GATHER_SEMS * 3),
         ],
         compiler_params=pltpu.CompilerParams(
@@ -548,7 +569,7 @@
 
 def body(factor):
     q, qt, note, m, basis = first_round(factor, 512)
-    rotated, w = rounds(factor, q, qt, m, note, 88)
+    rotated, w = rounds(factor, q, qt, m, note, 80)
     return finish(rotated.reshape(factor.shape), w, basis, 8)
 
 

time: 120 us -> 97.9 us (0.82)
  Pallas kernels: 118 us -> 95.4 us
    pallas_call x1, Pallas kernels: 105 us -> 82.6 us  [rounds(): pl.pallas_call(round_kernel, out_shape=(jax.ShapeDtypeStruct((2, order //...]
where the time goes in v4:
time: 97.9 us; the launch traced here: 96 us
  Pallas kernels  95.4 us (97%)
    pallas_call x1, Pallas kernels, rounds(): pl.pallas_call(round_kernel, out_shape=(jax.ShapeDtypeStruct((2, order //...  82.6 us
    pallas_call x1, Pallas kernels, first_round(): pl.pallas_call(first_kernel, out_shape=(square, square, square, square, j...  8.21 us
    pallas_call x1, Pallas kernels, finish(): pl.pallas_call(finish_kernel, out_shape=(shape, shape), in_specs=[HBM, VM...  4.55 us

profile of v4, /device:TPU:2, one launch (start us, length us, event | category | flops | bytes accessed | tf_op | source)
XLA Modules:
  0.0 96.0 jit_solution(11778209909752871534)
XLA Ops:
  0.6 8.2 %first_round.1 = (f32[128,128]{1,0:T(8,128)}, f32[128,128]{1,0:T(8,128)}, f32[128,128]{1,0:T(8,128)}, f32[128,128]{1,0:T(8,128)}, f32[8192,128]{1,0:T(8,128)}) custom-call(f32[8192,128]{1,0:T(8,128)} %a_ref.3), custom_call_target="tpu_custom_call" | custom-call | flops 1000000000 | bytes 10000000 | tf_op jit(solution)/shard_map/first_round/pallas_call | solution.py:125
  8.8 82.6 %rounds.1 = (f32[2,4096,128]{2,1,0:T(8,128)}, f32[2,128,128]{2,1,0:T(8,128)}) custom-call(f32[8192,128]{1,0:T(8,128)} %a_ref.3, f32[128,128]{1,0:T(8,128)} %get-tuple-element.9.q_ref, f32[128,128]{1,0:T(8,128)} %get-tuple-element.10.qt_ref, f32[128,128]{1,0:T(8,128)} %get-tuple-element.11.m_ref, f32[128,128]{1,0:T(8,128)} %get-tuple-element.12.note_ref), custom_call_target="tpu_custom_call" | custom-call | flops 10000000000 | bytes 10000000 | tf_op jit(solution)/shard_map/rounds/pallas_call | solution.py:486
  91.5 4.5 %finish.1 = (f32[8192,128]{1,0:T(8,128)}, f32[8192,128]{1,0:T(8,128)}) custom-call(f32[8192,128]{1,0:T(8,128)} %bitcast.1, f32[2,128,128]{2,1,0:T(8,128)} %get-tuple-element.14.w_ref, f32[8192,128]{1,0:T(8,128)} %get-tuple-element.15.zero_ref), custom_call_target="tpu_custom_call", output_to_operand_aliasing={{1}: (2, {})} | custom-call | flops 1000000 | bytes 10000000 | tf_op jit(solution)/shard_map/finish/pallas_call | solution.py:552

commit v5 on v4

--- a/solution.py
+++ b/solution.py
@@ -271,9 +271,9 @@
 
 def round_kernel(
     a_ref, q_ref, qt_ref, m_ref, note_ref,
-    out_ref, w_ref,
-    first, second, third, held, send, recv, keep, z_ref, q_pair, turn_pair, note, upper_ref, lower_ref,
-    local_sem, note_sem, bulk_sem, ready_sem, *gather_sems,
+    put_ref, w_ref,
+    out_ref, first, second, third, held, send, recv, keep, z_ref, q_pair, turn_pair, note, upper_ref, lower_ref,
+    local_sem, note_sem, bulk_sem, ready_sem, put_sem, *gather_sems,
 ):
     span = q_ref.shape[0]
     half = span // 2
@@ -398,6 +398,18 @@
         for step in range(4):
             x_at, z_at = lax.rem(x + step, 4), three.plane(r)
             far(third.at[z_at, x_at], cut, span - cut, x_at, z_at)
+
+    put = []
+
+    def put_out(r):
+        for b in range(2):
+            at = rows_at(4 * b + one.plane(r), size)
+            for side in range(2):
+                copy = pltpu.make_async_copy(
+                    out_ref.at[side, at], put_ref.at[side, at], put_sem.at[r, b, side]
+                )
+                copy.start()
+                put.append(copy)
 
     three.drain()
     two.drain()
@@ -465,12 +477,17 @@
         two.x_near(r)
         two.x_far(r)
         far_ring(r, range(4))
+    for r in (0, 1, 2):
+        put_out(r)
     two.x_near(3)
     far_ring(3, (0, 1, 3))
     three.z_end(3)
     far_line(3)
     two.x_far(3)
     far_ring(3, (2,))
+    put_out(3)
+    for copy in put:
+        copy.wait()
     told.wait_send()
     for copy in bulk:
         copy.wait_send()
@@ -490,8 +507,9 @@
             jax.ShapeDtypeStruct((2, span, span), f32),
         ),
         in_specs=[HBM, VMEM, VMEM, VMEM, VMEM],
-        out_specs=[VMEM, VMEM],
+        out_specs=[HBM, VMEM],
         scratch_shapes=[
+            pltpu.VMEM((2, order // 2, span), f32),
             pltpu.VMEM((4, 4, 4, span, span), f32),
             pltpu.VMEM((4, 4, 4, cut, span), f32),
             pltpu.VMEM((4, 4, 4, span - cut, span), f32),
@@ -505,6 +523,7 @@
             pltpu.SemaphoreType.DMA((2,)),
             pltpu.SemaphoreType.DMA((2, 4, 2)),
             pltpu.SemaphoreType.REGULAR,
+            pltpu.SemaphoreType.DMA((4, 2, 2)),
             *(GATHER_SEMS * 3),
         ],
         compiler_params=pltpu.CompilerParams(
@@ -569,8 +588,8 @@
 
 def body(factor):
     q, qt, note, m, basis = first_round(factor, 512)
-    rotated, w = rounds(factor, q, qt, m, note, 80)
-    return finish(rotated.reshape(factor.shape), w, basis, 8)
+    rotated, w = rounds(factor, q, qt, m, note, 72)
+    return finish(rotated.reshape(factor.shape), w, basis, 4)
 
 
 def solution(mesh):

time: 97.9 us -> 96.9 us (0.990)
  the two profiles are of different devices: /device:TPU:2 before, /device:TPU:128 now
where the time goes in v5:
time: 96.9 us; the launch traced here: 96.5 us
  Pallas kernels  95.9 us (99%)
    pallas_call x1, Pallas kernels, rounds(): pl.pallas_call(round_kernel, out_shape=(jax.ShapeDtypeStruct((2, order //...  83.2 us
    pallas_call x1, Pallas kernels, first_round(): pl.pallas_call(first_kernel, out_shape=(square, square, square, square, j...  8.4 us
    pallas_call x1, Pallas kernels, finish(): pl.pallas_call(finish_kernel, out_shape=(shape, shape), in_specs=[HBM, VM...  4.27 us

profile of v5, /device:TPU:128, one launch (start us, length us, event | category | flops | bytes accessed | tf_op | source)
XLA Modules:
  0.0 96.5 jit_solution(10845796328496425096)
XLA Ops:
  0.6 8.4 %first_round.1 = (f32[128,128]{1,0:T(8,128)}, f32[128,128]{1,0:T(8,128)}, f32[128,128]{1,0:T(8,128)}, f32[128,128]{1,0:T(8,128)}, f32[8192,128]{1,0:T(8,128)}) custom-call(f32[8192,128]{1,0:T(8,128)} %a_ref.3), custom_call_target="tpu_custom_call" | custom-call | flops 1000000000 | bytes 10000000 | tf_op jit(solution)/shard_map/first_round/pallas_call | solution.py:125
  9.0 83.2 %rounds.1 = (f32[2,4096,128]{2,1,0:T(8,128)}, f32[2,128,128]{2,1,0:T(8,128)}) custom-call(f32[8192,128]{1,0:T(8,128)} %a_ref.3, f32[128,128]{1,0:T(8,128)} %get-tuple-element.9.q_ref, f32[128,128]{1,0:T(8,128)} %get-tuple-element.10.qt_ref, f32[128,128]{1,0:T(8,128)} %get-tuple-element.11.m_ref, f32[128,128]{1,0:T(8,128)} %get-tuple-element.12.note_ref), custom_call_target="tpu_custom_call" | custom-call | flops 10000000000 | bytes 10000000 | tf_op jit(solution)/shard_map/rounds/pallas_call | solution.py:503
  92.3 4.3 %finish.1 = (f32[8192,128]{1,0:T(8,128)}, f32[8192,128]{1,0:T(8,128)}) custom-call(f32[8192,128]{1,0:T(8,128)} %bitcast.1, f32[2,128,128]{2,1,0:T(8,128)} %get-tuple-element.14.w_ref, f32[8192,128]{1,0:T(8,128)} %get-tuple-element.15.zero_ref), custom_call_target="tpu_custom_call", output_to_operand_aliasing={{1}: (2, {})} | custom-call | flops 1000000 | bytes 10000000 | tf_op jit(solution)/shard_map/finish/pallas_call | solution.py:571
